TPU v7x, 32 devices: a whole 2x2x4 slice. The times are simulated.
32 devices in a mesh: epoch: 8 (over z, y), blend: 4 (over x, core).
Axes of the slice: x: 2, y: 2, z: 4, core: 2. Of those that a mesh axis runs over, the one named last changes fastest.
Arguments:
- models: float32 [4, 16, 6, 4096], P('blend', 'epoch'), may hold values from -6 to 6
- observed: bfloat16 [8, 64, 4096], P('epoch', 'blend'), may hold values from -6 to 6
- weights: float32 [8, 64], P('epoch', 'blend'), may hold values from 0.5 to 2
- coverage: int32 [8, 64], P('epoch', 'blend'), may hold values from 0 to 1, as said below
- offsets: int32 [8, 64, 2], P('epoch', 'blend'), may hold values from 0 to 63
- counts: int32 [4, 16], P('blend', 'epoch'), may hold values from 1 to 8, as said below
- psf_y: bfloat16 [8, 4096], P('epoch'), may hold values from -0.75 to 0.75
- resample_y: bfloat16 [8, 4096], P('epoch'), may hold values from -0.75 to 0.75
- psf_x: bfloat16 [8, 4096], P('epoch'), may hold values from -0.75 to 0.75
- resample_x: bfloat16 [8, 4096], P('epoch'), may hold values from -0.75 to 0.75
Outputs:
- updated: float32 [4, 16, 6, 4096], P('blend', 'epoch')
Inputs may be any that keep to these rules, and one draw needn't show every extreme that they name: `coverage`: every blend is seen by one epoch or more. counts of blend b is the sum of coverage over all epochs for b.
All inputs are finite; a program needn't handle non-finite values.
Results may differ from a plain program's by a relative error of at most 0.0017.
Values may be sent and summed in bfloat16 or wider, within the bound.
A program may use at most 128 MiB of HBM per device.

v0:
```python
import jax
import jax.numpy as jnp
from jax import lax
from jax.sharding import PartitionSpec as P

CUT = 64
BANDS = 6
PIX2 = 4096
step_size = 0.5


def roll_forward(image, down, across):
    side = image.shape[0]
    doubled = jnp.concatenate([image, image], axis=0)
    rows = lax.dynamic_slice_in_dim(doubled, down, side, 0)
    doubled = jnp.concatenate([rows, rows], axis=1)
    return lax.dynamic_slice_in_dim(doubled, across, side, 1)


def one_epoch(model_low, observed, scale, offsets, left, right, band):
    side = left.shape[0]
    count = observed.shape[0]
    chosen = lax.dynamic_index_in_dim(model_low, band, 1, keepdims=False)
    shifted = jax.vmap(roll_forward)(chosen, offsets[:, 0], offsets[:, 1])
    blurred = jnp.einsum("ij,bjk->bik", left, shifted, preferred_element_type=jnp.float32).astype(
        jnp.bfloat16
    )
    predicted = jnp.einsum("bik,lk->bil", blurred, right, preferred_element_type=jnp.float32)
    target = observed.reshape(count, side, side).astype(jnp.float32)
    misfit = (scale[:, None, None] * (predicted - target)).astype(jnp.bfloat16)
    back = jnp.einsum("ji,bjk->bik", left, misfit, preferred_element_type=jnp.float32).astype(
        jnp.bfloat16
    )
    term = jnp.einsum("bik,kl->bil", back, right, preferred_element_type=jnp.float32)
    return jax.vmap(roll_forward)(term, side - offsets[:, 0], side - offsets[:, 1])


def on_device(
    models, observed, weights, coverage, offsets, counts, psf_y, resample_y, psf_x, resample_x
):
    ep_dev = observed.shape[0]
    group_size = lax.axis_size("epoch")
    all_epochs = ep_dev * group_size
    anchor = lax.axis_index("epoch") * ep_dev
    lefts = jnp.einsum(
        "eij,ejk->eik",
        psf_y.reshape(ep_dev, CUT, CUT),
        resample_y.reshape(ep_dev, CUT, CUT),
        preferred_element_type=jnp.float32,
    ).astype(jnp.bfloat16)
    rights = jnp.einsum(
        "eij,ejk->eik",
        psf_x.reshape(ep_dev, CUT, CUT),
        resample_x.reshape(ep_dev, CUT, CUT),
        preferred_element_type=jnp.float32,
    ).astype(jnp.bfloat16)
    scale = weights * coverage.astype(jnp.float32)
    epoch_bands = (anchor + 0) * BANDS // all_epochs
    first_band = anchor * BANDS // all_epochs
    model_low = models.astype(jnp.bfloat16)
    piece = lax.all_gather(model_low, "epoch", axis=1, tiled=True)
    count = piece.shape[1]
    blocks = piece[0].reshape(count, BANDS, CUT, CUT)
    terms = one_epoch(
        blocks, observed[0], scale[0], offsets[0], lefts[0], rights[0], epoch_bands
    ).reshape(count, PIX2)
    total = jnp.zeros((count, 2, PIX2), jnp.float32)
    slot = epoch_bands - first_band
    current = lax.dynamic_index_in_dim(total, slot, 1, keepdims=False)
    total = lax.dynamic_update_index_in_dim(total, current + terms, slot, 1)
    received = lax.all_to_all(total, "epoch", split_axis=0, concat_axis=1, tiled=True)
    slot_count = received.shape[1]
    position = jnp.arange(slot_count, dtype=jnp.int32)
    source = position // 2
    band_of = source * ep_dev * BANDS // all_epochs + position % 2
    selector = (band_of[:, None] == jnp.arange(BANDS, dtype=jnp.int32)[None, :]).astype(jnp.float32)
    gradient = jnp.einsum("bkp,kc->bcp", received, selector, precision=lax.Precision.HIGHEST)
    divisor = counts[0].astype(jnp.float32)[:, None, None]
    updated = models[0] - step_size * gradient / divisor
    return updated[None]


def solution(mesh):
    return jax.shard_map(
        on_device,
        mesh=mesh,
        in_specs=(
            P("blend", "epoch", None, None),
            P("epoch", "blend", None),
            P("epoch", "blend"),
            P("epoch", "blend"),
            P("epoch", "blend", None),
            P("blend", "epoch"),
            P("epoch", None),
            P("epoch", None),
            P("epoch", None),
            P("epoch", None),
        ),
        out_specs=P("blend", "epoch", None, None),
        check_vma=False,
    )
```

profile of v0, /device:TPU:0, one launch (start us, length us, event | category | flops | bytes accessed | tf_op | source)
XLA Modules:
  0.0 66.9 jit_solution(17146201242047359278)
XLA Ops:
  0.0 1.0 %convert_element_type.47 = bf16[1,2,6,4096]{3,1,2,0:T(2,128)(2,1)S(1)} convert(f32[1,2,6,4096]{3,1,2,0:T(2,128)} %param.10) | non-fusion elementwise | flops 49152 | bytes 294912 | tf_op jit(solution)/shard_map/convert_element_type | solution.py:60
  1.0 0.1 copy.60
  1.1 34.6 %all_gather.3 = bf16[1,16,6,4096]{3,2,0,1:T(8,128)(2,1)S(1)} all-gather(bf16[1,2,6,4096]{3,2,0,1:T(8,128)(2,1)S(1)} %copy.60), channel_id=1, replica_groups=mesh['epoch'=8,'blend'=4] {'epoch'}, dimensions={1}, use_global_device_ids=true | all-gather | bytes 884736 | tf_op jit(solution)/shard_map/all_gather | solution.py:61
  35.7 0.4 copy.61
  36.1 0.0 copy-start.6
  36.1 1.7 %reshape_squeeze.4 = bf16[16,6,64,64]{3,2,0,1:T(8,128)(2,1)S(1)} reshape(bf16[1,16,6,4096]{3,1,2,0:T(8,128)(2,1)S(1)} %copy.61) | data formatting | bytes 1572864 | tf_op jit(solution)/shard_map/reshape;squeeze | solution.py:63
  37.9 0.2 copy.86
  38.1 0.1 pad_maximum_fusion
  38.2 0.0 copy-done.6
  38.2 0.0 copy-start.2
  38.2 0.0 copy-start.3
  38.2 0.0 copy-start.4
  38.2 0.0 copy-start.5
  38.3 0.0 copy-start.1
  38.3 1.4 %gather_fusion = bf16[16,64,64]{2,0,1:T(8,128)(2,1)S(1)} fusion(bf16[16,128,64]{2,0,1:T(8,128)(2,1)S(1)} %pad_maximum_fusion, s32[16]{0:T(128)S(1)} %get-tuple-element.6), kind=kCustom, calls=%fused_computation | custom fusion | bytes 262336 | tf_op jit(solution)/shard_map/vmap()/gather | solution.py:15
  39.6 0.1 pad_maximum_fusion.3
  39.8 0.5 copy.63
  40.4 0.1 reduce.2
  40.4 0.1 reshape.76
  40.5 0.1 reduce.3
  40.5 0.1 reshape.77
  40.6 0.1 reduce
  40.7 0.1 reshape.74
  40.8 0.1 reduce.1
  40.8 0.0 copy-start.7
  40.8 0.0 copy-start.8
  40.9 0.1 reshape.75
  40.9 0.2 reshape.78
  41.2 1.4 %gather_fusion.1 = bf16[16,64,64]{1,0,2:T(8,128)(2,1)S(1)} fusion(bf16[16,64,128]{1,0,2:T(8,128)(2,1)S(1)} %copy.63, s32[16]{0:T(128)S(1)} %get-tuple-element.7), kind=kCustom, calls=%fused_computation.1 | custom fusion | bytes 262336 | tf_op jit(solution)/shard_map/vmap()/gather | solution.py:17
  42.5 0.1 fusion.10
  42.7 0.1 fusion.9
  42.8 0.4 fusion.5
  43.3 0.4 fusion.8
  43.7 0.2 pad_maximum_fusion.1
  43.9 0.5 copy.69
  44.4 1.3 %gather_fusion.2 = f32[16,64,64]{2,0,1:T(8,128)S(1)} fusion(f32[16,128,64]{2,0,1:T(8,128)S(1)} %copy.69, s32[16]{0:T(128)S(1)} %get-tuple-element.8), kind=kCustom, calls=%fused_computation.2 | custom fusion | bytes 524480 | tf_op jit(solution)/shard_map/vmap()/gather | solution.py:15
  45.8 0.2 pad_maximum_fusion.2
  46.0 0.6 copy.70
  46.6 1.3 %gather_fusion.3 = f32[16,64,64]{1,0,2:T(8,128)S(1)} fusion(f32[16,64,128]{1,0,2:T(8,128)S(1)} %copy.70, s32[16]{0:T(128)S(1)} %get-tuple-element.5), kind=kCustom, calls=%fused_computation.3 | custom fusion | bytes 524480 | tf_op jit(solution)/shard_map/vmap()/gather | solution.py:17
  47.9 0.3 copy.71
  48.2 0.0 copy-start.9
  48.2 0.3 broadcast_in_dim.8
  48.5 1.0 %dynamic_update_slice.4.clone = f32[16,2,4096]{2,1,0:T(2,128)} pad(f32[16,1,4096]{2,1,0:T(1,128)S(1)} %broadcast_in_dim.8, f32[]{:T(128)} %constant.85.clone.1), padding=0_0x0_1x0_0 | pad | bytes 786436 | tf_op jit(solution)/shard_map/jit(dynamic_update_index_in_dim)/dynamic_update_slice | solution.py:70
  49.5 5.5 %all-to-all-start = ((f32[16,2,4096]{2,1,0:T(2,128)}), f32[16,2,4096]{2,1,0:T(2,128)S(1)}, u32[]{:S(2)}, u32[]{:S(2)}) async-start(f32[16,2,4096]{2,1,0:T(2,128)} %dynamic_update_slice.4.clone), calls=%async_computation | async-start | bytes 1048576 | tf_op jit(solution)/shard_map/all_to_all | solution.py:71
  55.0 10.3 %all-to-all-done = f32[16,2,4096]{2,1,0:T(2,128)S(1)} async-done(((f32[16,2,4096]{2,1,0:T(2,128)}), f32[16,2,4096]{2,1,0:T(2,128)S(1)}, u32[]{:S(2)}, u32[]{:S(2)}) %all-to-all-start) | async-done | bytes 524320 | tf_op jit(solution)/shard_map/all_to_all | solution.py:71
  65.3 0.4 all_to_all.16
  65.7 0.4 fusion.3
  66.1 0.8 %copy.74 = f32[1,2,6,4096]{3,1,2,0:T(2,128)} copy(f32[1,2,6,4096]{3,2,1,0:T(8,128)S(1)} %fusion.3) | data formatting | bytes 393216 | tf_op jit(solution)/shard_map/broadcast_in_dim | solution.py:80
  (16 shorter events, 0.1 us)
Async XLA Ops:
  36.1 2.1 %copy-start.6 = (s32[1,16,2]{1,2,0:T(2,128)S(1)}, s32[1,16,2]{1,2,0:T(2,128)}, u32[]{:S(2)}) copy-start(s32[1,16,2]{1,2,0:T(2,128)} %param.14) | copy-start | bytes 388
  38.2 2.1 %copy-start.2 = (bf16[1,4096]{1,0:T(2,128)(2,1)S(1)}, bf16[1,4096]{1,0:T(2,128)(2,1)}, u32[]{:S(2)}) copy-start(bf16[1,4096]{1,0:T(2,128)(2,1)} %param.18) | copy-start | bytes 24580
  38.2 2.3 %copy-start.3 = (bf16[1,4096]{1,0:T(2,128)(2,1)S(1)}, bf16[1,4096]{1,0:T(2,128)(2,1)}, u32[]{:S(2)}) copy-start(bf16[1,4096]{1,0:T(2,128)(2,1)} %param.19) | copy-start | bytes 24580
  38.2 2.4 %copy-start.4 = (bf16[1,4096]{1,0:T(2,128)(2,1)S(1)}, bf16[1,4096]{1,0:T(2,128)(2,1)}, u32[]{:S(2)}) copy-start(bf16[1,4096]{1,0:T(2,128)(2,1)} %param.16) | copy-start | bytes 24580
  38.2 2.5 %copy-start.5 = (bf16[1,4096]{1,0:T(2,128)(2,1)S(1)}, bf16[1,4096]{1,0:T(2,128)(2,1)}, u32[]{:S(2)}) copy-start(bf16[1,4096]{1,0:T(2,128)(2,1)} %param.17) | copy-start | bytes 24580
  38.3 2.7 %copy-start.1 = (bf16[1,16,4096]{2,1,0:T(8,128)(2,1)S(1)}, bf16[1,16,4096]{2,1,0:T(8,128)(2,1)}, u32[]{:S(2)}) copy-start(bf16[1,16,4096]{2,1,0:T(8,128)(2,1)} %param.11) | copy-start | bytes 393220
  40.8 2.0 %copy-start.7 = (f32[1,16]{1,0:T(1,128)S(1)}, f32[1,16]{1,0:T(1,128)}, u32[]{:S(2)}) copy-start(f32[1,16]{1,0:T(1,128)} %param.12) | copy-start | bytes 196
  40.8 1.9 %copy-start.8 = (s32[1,16]{1,0:T(1,128)S(1)}, s32[1,16]{1,0:T(1,128)}, u32[]{:S(2)}) copy-start(s32[1,16]{1,0:T(1,128)} %param.13) | copy-start | bytes 196
  48.2 6.9 %copy-start.9 = (s32[1,2]{1,0:T(1,128)S(1)}, s32[1,2]{1,0:T(1,128)}, u32[]{:S(2)}) copy-start(s32[1,2]{1,0:T(1,128)} %param.15) | copy-start | bytes 28
  49.5 16.2 %copy-start = (f32[1,2,6,4096]{3,1,2,0:T(2,128)S(1)}, f32[1,2,6,4096]{3,1,2,0:T(2,128)}, u32[]{:S(2)}) copy-start(f32[1,2,6,4096]{3,1,2,0:T(2,128)} %param.10) | copy-start | bytes 589828
  49.5 15.8 %all-to-all-start = ((f32[16,2,4096]{2,1,0:T(2,128)}), f32[16,2,4096]{2,1,0:T(2,128)S(1)}, u32[]{:S(2)}, u32[]{:S(2)}) async-start(f32[16,2,4096]{2,1,0:T(2,128)} %dynamic_update_slice.4.clone), calls=%async_computation | async-start | bytes 1048576 | tf_op jit(solution)/shard_map/all_to_all | solution.py:71
where the time goes:
time: 67.1 us; the launch traced here: 66.9 us
  blocking collectives  34.6 us (52%)
  local copies, waits for them, and re-layouts  12.8 us (19%)
  waiting for transfers between devices  10.3 us (15%)
  starting transfers between devices  5.52 us (8%)
  other arithmetic  1.9 us (3%)
  matrix products  1.48 us (2%)
    all_gather x1, blocking collectives, on_device(): piece = lax.all_gather(model_low, 'epoch', axis=1, tiled=True)  34.6 us
    all_to_all x1, waiting for transfers between devices, on_device(): lax.all_to_all(total, 'epoch', split_axis=0, concat_axis=1, tiled=True)  10.3 us
    all_to_all x1, starting transfers between devices, on_device(): lax.all_to_all(total, 'epoch', split_axis=0, concat_axis=1, tiled=True)  5.52 us
    gather x3, local copies, waits for them, and re-layouts, roll_forward(): return lax.dynamic_slice_in_dim(doubled, across, side, 1)  2.97 us
    gather x2, local copies, waits for them, and re-layouts, roll_forward(): rows = lax.dynamic_slice_in_dim(doubled, down, side, 0)  2.71 us
    another operation x1, local copies, waits for them, and re-layouts, on_device(): blocks = piece[0].reshape(count, BANDS, CUT, CUT)  1.72 us
  transfers between devices with their start and end apart: 1, of which 1 were waited for; matrix products, arithmetic and copies ran while one was open for 0% of the time, Pallas kernels for 0%

commit v1 on v0

--- a/solution.py
+++ b/solution.py
@@ -68,7 +68,10 @@
     slot = epoch_bands - first_band
     current = lax.dynamic_index_in_dim(total, slot, 1, keepdims=False)
     total = lax.dynamic_update_index_in_dim(total, current + terms, slot, 1)
-    received = lax.all_to_all(total, "epoch", split_axis=0, concat_axis=1, tiled=True)
+    received = jnp.concatenate(
+        lax.all_to_all(jnp.stack(jnp.split(total, lax.axis_size("epoch"), axis=0)), "epoch", 0, 0),
+        axis=1,
+    )
     slot_count = received.shape[1]
     position = jnp.arange(slot_count, dtype=jnp.int32)
     source = position // 2

time: 67.1 us -> 70.9 us (1.057)
  local copies, waits for them, and re-layouts: 12.8 us -> 16.4 us
    unnamed x20 -> x27, local copies, waits for them, and re-layouts: 0.06 us -> 4.53 us
    dynamic_update_slice x1 -> x0, local copies, waits for them, and re-layouts: 0.99 us -> none  [on_device(): total = lax.dynamic_update_index_in_dim(total, current + terms, slot, 1)]
where the time goes in v1:
time: 70.9 us; the launch traced here: 70.6 us
  blocking collectives  34.6 us (49%)
  local copies, waits for them, and re-layouts  16.4 us (23%)
  waiting for transfers between devices  10.3 us (15%)
  starting transfers between devices  5.39 us (8%)
  other arithmetic  1.9 us (3%)
  matrix products  1.78 us (3%)
    all_gather x1, blocking collectives, on_device(): piece = lax.all_gather(model_low, 'epoch', axis=1, tiled=True)  34.6 us
    all_to_all x1, waiting for transfers between devices, on_device(): lax.all_to_all(jnp.stack(jnp.split(total, lax.axis_size('epoch'), axis=0)...  10.3 us
    all_to_all x1, starting transfers between devices, on_device(): lax.all_to_all(jnp.stack(jnp.split(total, lax.axis_size('epoch'), axis=0)...  5.39 us
    unnamed x27, local copies, waits for them, and re-layouts  4.53 us
    gather x3, local copies, waits for them, and re-layouts, roll_forward(): return lax.dynamic_slice_in_dim(doubled, across, side, 1)  2.97 us
    gather x2, local copies, waits for them, and re-layouts, roll_forward(): rows = lax.dynamic_slice_in_dim(doubled, down, side, 0)  2.71 us
    another operation x1, local copies, waits for them, and re-layouts, on_device(): blocks = piece[0].reshape(count, BANDS, CUT, CUT)  1.72 us
  transfers between devices with their start and end apart: 1, of which 1 were waited for; matrix products, arithmetic and copies ran while one was open for 0% of the time, Pallas kernels for 0%

profile of v1, /device:TPU:0, one launch (start us, length us, event | category | flops | bytes accessed | tf_op | source)
XLA Modules:
  0.0 70.6 jit_solution(10355427787271316890)
XLA Ops:
  0.0 1.0 %convert_element_type.47 = bf16[1,2,6,4096]{3,1,2,0:T(2,128)(2,1)S(1)} convert(f32[1,2,6,4096]{3,1,2,0:T(2,128)} %param.10) | non-fusion elementwise | flops 49152 | bytes 294912 | tf_op jit(solution)/shard_map/convert_element_type | solution.py:60
  1.0 0.1 copy.64
  1.1 34.6 %all_gather.3 = bf16[1,16,6,4096]{3,2,0,1:T(8,128)(2,1)S(1)} all-gather(bf16[1,2,6,4096]{3,2,0,1:T(8,128)(2,1)S(1)} %copy.64), channel_id=1, replica_groups=mesh['epoch'=8,'blend'=4] {'epoch'}, dimensions={1}, use_global_device_ids=true | all-gather | bytes 884736 | tf_op jit(solution)/shard_map/all_gather | solution.py:61
  35.7 0.4 copy.65
  36.1 1.7 %reshape_squeeze.4 = bf16[16,6,64,64]{3,2,0,1:T(8,128)(2,1)S(1)} reshape(bf16[1,16,6,4096]{3,1,2,0:T(8,128)(2,1)S(1)} %copy.65) | data formatting | bytes 1572864 | tf_op jit(solution)/shard_map/reshape;squeeze | solution.py:63
  37.9 0.2 copy.91
  38.1 0.1 pad_maximum_fusion
  38.2 0.0 copy-start.3
  38.2 0.0 copy-start.4
  38.3 1.4 %gather_fusion = bf16[16,64,64]{2,0,1:T(8,128)(2,1)S(1)} fusion(bf16[16,128,64]{2,0,1:T(8,128)(2,1)S(1)} %pad_maximum_fusion, s32[16]{0:T(128)S(1)} %get-tuple-element.6), kind=kCustom, calls=%fused_computation | custom fusion | bytes 262336 | tf_op jit(solution)/shard_map/vmap()/gather | solution.py:15
  39.6 0.1 pad_maximum_fusion.3
  39.8 0.5 copy.67
  40.4 0.1 reduce.2
  40.4 0.1 reshape.82
  40.5 0.1 reduce.3
  40.5 0.1 reshape.83
  40.6 0.1 reduce
  40.7 0.1 reshape.80
  40.8 0.1 reduce.1
  40.8 0.0 copy-start.7
  40.8 0.0 copy-start.8
  40.9 0.1 reshape.81
  40.9 0.2 reshape.86
  41.2 1.4 %gather_fusion.1 = bf16[16,64,64]{1,0,2:T(8,128)(2,1)S(1)} fusion(bf16[16,64,128]{1,0,2:T(8,128)(2,1)S(1)} %copy.67, s32[16]{0:T(128)S(1)} %get-tuple-element.7), kind=kCustom, calls=%fused_computation.1 | custom fusion | bytes 262336 | tf_op jit(solution)/shard_map/vmap()/gather | solution.py:17
  42.5 0.1 fusion.10
  42.7 0.1 fusion.9
  42.8 0.4 fusion.5
  43.3 0.4 fusion.8
  43.7 0.2 pad_maximum_fusion.1
  43.9 0.5 copy.73
  44.4 1.3 %gather_fusion.2 = f32[16,64,64]{2,0,1:T(8,128)S(1)} fusion(f32[16,128,64]{2,0,1:T(8,128)S(1)} %copy.73, s32[16]{0:T(128)S(1)} %get-tuple-element.8), kind=kCustom, calls=%fused_computation.2 | custom fusion | bytes 524480 | tf_op jit(solution)/shard_map/vmap()/gather | solution.py:15
  45.8 0.2 pad_maximum_fusion.2
  46.0 0.6 copy.74
  46.6 1.3 %gather_fusion.3 = f32[16,64,64]{1,0,2:T(8,128)S(1)} fusion(f32[16,64,128]{1,0,2:T(8,128)S(1)} %copy.74, s32[16]{0:T(128)S(1)} %get-tuple-element.5), kind=kCustom, calls=%fused_computation.3 | custom fusion | bytes 524480 | tf_op jit(solution)/shard_map/vmap()/gather | solution.py:17
  47.9 0.3 copy.75
  48.2 0.2 broadcast_in_dim.5
  48.3 0.6 fusion.15
  49.0 0.6 fusion.17
  49.6 0.6 fusion.19
  50.3 0.6 fusion.21
  50.9 0.6 fusion.23
  51.5 0.6 fusion.25
  52.2 0.6 fusion.27
  52.8 0.6 fusion.29
  53.5 5.4 %all-to-all-start = ((f32[8,2,2,4096]{3,1,2,0:T(2,128)}), f32[8,2,2,4096]{3,1,2,0:T(2,128)S(1)}, u32[]{:S(2)}, u32[]{:S(2)}) async-start(f32[8,2,2,4096]{3,1,2,0:T(2,128)} %fusion.29), calls=%async_computation | async-start | bytes 1048576 | tf_op jit(solution)/shard_map/all_to_all | solution.py:72
  58.9 10.3 %all-to-all-done = f32[8,2,2,4096]{3,1,2,0:T(2,128)S(1)} async-done(((f32[8,2,2,4096]{3,1,2,0:T(2,128)}), f32[8,2,2,4096]{3,1,2,0:T(2,128)S(1)}, u32[]{:S(2)}, u32[]{:S(2)}) %all-to-all-start) | async-done | bytes 524320 | tf_op jit(solution)/shard_map/all_to_all | solution.py:72
  69.1 0.7 fusion.3
  69.8 0.8 %copy.77 = f32[1,2,6,4096]{3,1,2,0:T(2,128)} copy(f32[1,2,6,4096]{3,2,1,0:T(8,128)S(1)} %fusion.3) | data formatting | bytes 393216 | tf_op jit(solution)/shard_map/broadcast_in_dim | solution.py:83
  (21 shorter events, 0.1 us)
Async XLA Ops:
  36.1 2.1 %copy-start.6 = (s32[1,16,2]{1,2,0:T(2,128)S(1)}, s32[1,16,2]{1,2,0:T(2,128)}, u32[]{:S(2)}) copy-start(s32[1,16,2]{1,2,0:T(2,128)} %param.14) | copy-start | bytes 388
  38.2 2.1 %copy-start.2 = (bf16[1,4096]{1,0:T(2,128)(2,1)S(1)}, bf16[1,4096]{1,0:T(2,128)(2,1)}, u32[]{:S(2)}) copy-start(bf16[1,4096]{1,0:T(2,128)(2,1)} %param.18) | copy-start | bytes 24580
  38.2 2.3 %copy-start.3 = (bf16[1,4096]{1,0:T(2,128)(2,1)S(1)}, bf16[1,4096]{1,0:T(2,128)(2,1)}, u32[]{:S(2)}) copy-start(bf16[1,4096]{1,0:T(2,128)(2,1)} %param.19) | copy-start | bytes 24580
  38.2 2.4 %copy-start.4 = (bf16[1,4096]{1,0:T(2,128)(2,1)S(1)}, bf16[1,4096]{1,0:T(2,128)(2,1)}, u32[]{:S(2)}) copy-start(bf16[1,4096]{1,0:T(2,128)(2,1)} %param.16) | copy-start | bytes 24580
  38.2 2.5 %copy-start.5 = (bf16[1,4096]{1,0:T(2,128)(2,1)S(1)}, bf16[1,4096]{1,0:T(2,128)(2,1)}, u32[]{:S(2)}) copy-start(bf16[1,4096]{1,0:T(2,128)(2,1)} %param.17) | copy-start | bytes 24580
  38.3 2.7 %copy-start.1 = (bf16[1,16,4096]{2,1,0:T(8,128)(2,1)S(1)}, bf16[1,16,4096]{2,1,0:T(8,128)(2,1)}, u32[]{:S(2)}) copy-start(bf16[1,16,4096]{2,1,0:T(8,128)(2,1)} %param.11) | copy-start | bytes 393220
  40.8 2.0 %copy-start.7 = (f32[1,16]{1,0:T(1,128)S(1)}, f32[1,16]{1,0:T(1,128)}, u32[]{:S(2)}) copy-start(f32[1,16]{1,0:T(1,128)} %param.12) | copy-start | bytes 196
  40.8 1.9 %copy-start.8 = (s32[1,16]{1,0:T(1,128)S(1)}, s32[1,16]{1,0:T(1,128)}, u32[]{:S(2)}) copy-start(s32[1,16]{1,0:T(1,128)} %param.13) | copy-start | bytes 196
  49.6 9.3 %copy-start.9 = (s32[1,2]{1,0:T(1,128)S(1)}, s32[1,2]{1,0:T(1,128)}, u32[]{:S(2)}) copy-start(s32[1,2]{1,0:T(1,128)} %param.15) | copy-start | bytes 28
  49.6 19.5 %copy-start = (f32[1,2,6,4096]{3,1,2,0:T(2,128)S(1)}, f32[1,2,6,4096]{3,1,2,0:T(2,128)}, u32[]{:S(2)}) copy-start(f32[1,2,6,4096]{3,1,2,0:T(2,128)} %param.10) | copy-start | bytes 589828
  53.5 15.7 %all-to-all-start = ((f32[8,2,2,4096]{3,1,2,0:T(2,128)}), f32[8,2,2,4096]{3,1,2,0:T(2,128)S(1)}, u32[]{:S(2)}, u32[]{:S(2)}) async-start(f32[8,2,2,4096]{3,1,2,0:T(2,128)} %fusion.29), calls=%async_computation | async-start | bytes 1048576 | tf_op jit(solution)/shard_map/all_to_all | solution.py:72
